TPU v7x, 256 devices: a whole 4x4x8 slice. The times are simulated.
256 devices in a mesh: dp: 32 (over y, z), mp: 8 (over x, core).
Axes of the slice: x: 4, y: 4, z: 8, core: 2. Of those that a mesh axis runs over, the one named last changes fastest.
Arguments:
- grad_parts: bfloat16 [32, 8, 1024, 1024], P('dp', 'mp'), may hold values from -10 to 10
- left_stat: float32 [8, 1024, 1024], P('mp', 'dp'), may hold values from -60 to 500, as said below
- right_stat: float32 [8, 1024, 1024], P('mp', 'dp'), may hold values from -60 to 500, as said below
- left_root: bfloat16 [8, 1024, 1024], P('mp', 'dp'), may hold values from -2 to 2
- right_root: bfloat16 [8, 1024, 1024], P('mp', 'dp'), may hold values from -2 to 2
- due: int32 [8, 2], P('mp'), may hold values 0 or 1
Outputs:
- update: bfloat16 [8, 1024, 1024], P('mp')
- left_new: float32 [8, 1024, 1024], P('mp', 'dp')
- right_new: float32 [8, 1024, 1024], P('mp', 'dp')
- left_out: bfloat16 [8, 1024, 1024], P('mp', 'dp')
- right_out: bfloat16 [8, 1024, 1024], P('mp', 'dp')
Inputs may be any that keep to these rules, and one draw needn't show every extreme that they name: `left_stat`: every block is positive definite. `right_stat`: every block is positive definite. `due`: 1 where that statistic of the block gets a new root in this step.
All inputs are finite; a program needn't handle non-finite values.
Results may differ from a plain program's by a relative error of at most 0.022.
Values may be sent and summed in bfloat16 or wider, within the bound.
No kernel may reach another device: no remote copies, remote signals or barrier semaphores. Data moves between devices by JAX's collectives and lax.ppermute only.
A program may use at most 64 MiB of HBM per device.

v0:
```python
import jax
import jax.numpy as jnp
from jax import lax
from jax.sharding import Mesh
from jax.sharding import PartitionSpec as P

DP = ("dp_0", "dp_1")
DP_MP = ("dp_0", "dp_1", "mp_0", "mp_1")
MP = ("mp_0", "mp_1")
epsilon = 1e-06
decay = 0.9


def scatter_axes(value, axes, dim):
    for axis in axes:
        value = lax.psum_scatter(value, axis, scatter_dimension=dim, tiled=True)
    return value


def by_axis(value, axes):
    for axis in axes:
        value = lax.psum(value, axis)
    return value


def swapped(value, axis, apart):
    mask = 2**apart
    pairs = [(source, source ^ mask) for source in range(lax.axis_size(axis))]
    return lax.ppermute(value, axis, pairs)


def in_order(tiles, dim):
    tiles = jnp.moveaxis(tiles, 0, dim)
    dims = tiles.shape
    return tiles.reshape(*dims[:dim], dims[dim] * dims[dim + 1], *dims[dim + 2 :])


def gather_packed(arrays, axis, dims):
    ravelled = jnp.concatenate([a.reshape(-1) for a in arrays])
    lines, at, done = (lax.all_gather(ravelled, axis), 0, [])
    for a, dim in zip(arrays, dims):
        tiles = lines[:, at : at + a.size].reshape(-1, *a.shape)
        done.append(in_order(tiles, dim))
        at += a.size
    return tuple(done)


def root_batch(whole):
    order_size = whole.shape[-1]
    traces = jnp.trace(whole, axis1=1, axis2=2)
    traces = jnp.where(traces > 0.0, traces, 1.0)
    scale_c = 4.0 * traces / order_size
    identity = jnp.eye(order_size, dtype=jnp.float32)
    initial = ((5.0 * identity[None] - whole / scale_c[:, None, None]) / 4.0).astype(jnp.bfloat16)
    square = jnp.einsum(
        "kij,kjl->kil", initial, initial, preferred_element_type=jnp.float32
    ).astype(jnp.bfloat16)
    fourth = jnp.einsum("kij,kjl->kil", square, square, preferred_element_type=jnp.float32).astype(
        jnp.bfloat16
    )
    combined = (5.0 * initial.astype(jnp.float32) - 4.0 * square.astype(jnp.float32)).astype(
        jnp.bfloat16
    )
    product = jnp.einsum("kij,kjl->kil", fourth, combined, preferred_element_type=jnp.float32)
    return (
        scale_c[:, None, None] ** (-0.25) * (5.0 * initial.astype(jnp.float32) - product) / 4.0
    ).astype(jnp.bfloat16)


def per_device(grad_parts, left_stat, right_stat, left_root, right_root, due):
    partial_value = grad_parts[0]
    grad_rows = (
        scatter_axes(partial_value.astype(jnp.float32).astype(jnp.bfloat16), DP, 1)
        .astype(jnp.float32)
        .astype(jnp.bfloat16)
    )
    local_blocks = grad_rows.shape[0]
    row_count = grad_rows.shape[1]
    order_size = grad_rows.shape[2]
    square_sum = jnp.sum(grad_rows.astype(jnp.float32) ** 2)
    grand_sum = by_axis(square_sum, DP_MP)
    entry_count = float(lax.axis_size(MP) * local_blocks * order_size * order_size)
    factor = 1.0 / jnp.sqrt(grand_sum / entry_count + epsilon)
    full_grad = lax.all_gather(grad_rows, DP, axis=1, tiled=True)
    row_start = lax.axis_index(DP) * row_count
    own_cols = lax.dynamic_slice_in_dim(full_grad, row_start, row_count, 2)
    left_prod = jnp.einsum("brk,bck->brc", grad_rows, full_grad, preferred_element_type=jnp.float32)
    right_prod = jnp.einsum("bkr,bkc->brc", own_cols, full_grad, preferred_element_type=jnp.float32)
    left_new = left_stat * decay + left_prod * ((1.0 - decay) / order_size)
    right_new = right_stat * decay + right_prod * ((1.0 - decay) / order_size)
    statistics = jnp.concatenate([left_new, right_new], 0)
    stat_count = statistics.shape[0]
    peer_index = lax.axis_index(DP)
    level_count = lax.axis_size(DP).bit_length() - 1
    split_levels = stat_count.bit_length() - 1
    gathered = statistics
    for level_now in range(level_count):
        bit_value = peer_index // (1 << level_now) % 2
        if level_now < split_levels:
            paired = gathered.reshape(gathered.shape[0] // 2, 2, gathered.shape[1], order_size)
            kept_part = jnp.where(bit_value == 0, paired[:, 0], paired[:, 1])
            sent_part = jnp.where(bit_value == 0, paired[:, 1], paired[:, 0])
        else:
            kept_part = gathered
            sent_part = gathered
        arrived = swapped(sent_part, DP, level_now)
        gathered = jnp.where(
            bit_value == 0,
            jnp.concatenate([kept_part, arrived], 1),
            jnp.concatenate([arrived, kept_part], 1),
        )
    identity_full = jnp.eye(order_size, dtype=jnp.float32)[None]
    is_owner = peer_index < stat_count
    spreading = root_batch(jnp.where(is_owner, gathered, identity_full))
    for level_now in reversed(range(level_count)):
        bit_value = peer_index // (1 << level_now) % 2
        half_rows = spreading.shape[1] // 2
        lower_half = spreading[:, :half_rows]
        upper_half = spreading[:, half_rows:]
        kept_part = jnp.where(bit_value == 0, lower_half, upper_half)
        sent_part = jnp.where(bit_value == 0, upper_half, lower_half)
        arrived = swapped(sent_part, DP, level_now)
        if level_now < split_levels:
            stacked = jnp.where(
                bit_value == 0,
                jnp.stack([kept_part, arrived], 1),
                jnp.stack([arrived, kept_part], 1),
            )
            spreading = stacked.reshape(stacked.shape[0] * 2, half_rows, order_size)
        else:
            spreading = jnp.where(bit_value == 0, kept_part, arrived)
    due_flags = due.T.reshape(-1)
    old_roots = jnp.concatenate([left_root, right_root], 0)
    roots_used = jnp.where(due_flags[:, None, None] == 1, spreading, old_roots)
    left_out = roots_used[:local_blocks]
    right_out = roots_used[local_blocks:]
    x_rows = jnp.einsum(
        "brk,bkc->brc", left_out, full_grad, preferred_element_type=jnp.float32
    ).astype(jnp.bfloat16)
    x_all, right_all = gather_packed((x_rows, right_out), DP, (1, 1))
    update = (
        jnp.einsum("brk,bkc->brc", x_all, right_all, preferred_element_type=jnp.float32) * factor
    ).astype(jnp.bfloat16)
    return (update, left_new, right_new, left_out, right_out)


def solution(mesh):
    torus = Mesh(mesh.devices.reshape(4, 8, 4, 2), ("dp_0", "dp_1", "mp_0", "mp_1"))
    in_specs = (
        P(DP, MP, None, None),
        P(MP, DP, None),
        P(MP, DP, None),
        P(MP, DP, None),
        P(MP, DP, None),
        P(MP, None),
    )
    out_specs = (
        P(MP, None, None),
        P(MP, DP, None),
        P(MP, DP, None),
        P(MP, DP, None),
        P(MP, DP, None),
    )
    return jax.shard_map(
        per_device, mesh=torus, in_specs=in_specs, out_specs=out_specs, check_vma=False
    )
```

profile of v0, /device:TPU:2, one launch (start us, length us, event | category | flops | bytes accessed | tf_op | source)
XLA Modules:
  0.0 457.1 jit_solution(17009621048570984813)
XLA Ops:
  8.0 37.8 %reduce-scatter.3.cloned.1.call-done = bf16[1,256,1024]{2,1,0:T(8,128)(2,1)} async-done(((bf16[1,1024,1024]{2,1,0:T(8,128)(2,1)}), bf16[1,256,1024]{2,1,0:T(8,128)(2,1)}) %reduce-scatter.3.cloned.1.call-update) | async-done | bytes 524304 | tf_op jit(solution)/shard_map/reduce_scatter | solution.py:16
  45.9 39.9 %reduce-scatter.5.cloned.1.call-done = bf16[1,32,1024]{2,1,0:T(8,128)(2,1)} async-done(((bf16[1,256,1024]{2,1,0:T(8,128)(2,1)}), bf16[1,32,1024]{2,1,0:T(8,128)(2,1)}) %reduce-scatter.5.cloned.1.call-update) | async-done | bytes 65552 | tf_op jit(solution)/shard_map/reduce_scatter | solution.py:16
  85.9 79.2 %all-gather.4.cloned.1.call-done = bf16[1,1024,1024]{2,1,0:T(8,128)(2,1)} async-done(((bf16[1,32,1024]{2,1,0:T(8,128)(2,1)}), bf16[1,1024,1024]{2,1,0:T(8,128)(2,1)}) %all-gather.4.cloned.1.call-update) | async-done | bytes 2097168 | tf_op jit(solution)/shard_map/all_gather | solution.py:84
  169.0 4.8 %collective-permute-done = f32[1,32,1024]{2,1,0:T(8,128)S(1)} collective-permute-done((f32[1,32,1024]{2,1,0:T(8,128)S(1)}, f32[1,32,1024]{2,1,0:T(8,128)S(1)}, u32[]{:S(2)}, u32[]{:S(2)}) %collective-permute-start) | collective-permute-done | bytes 131104 | tf_op jit(solution)/shard_map/ppermute | solution.py:29
  177.2 19.0 %collective-permute-done.1 = f32[1,64,1024]{2,1,0:T(8,128)S(1)} collective-permute-done((f32[1,64,1024]{2,1,0:T(8,128)}, f32[1,64,1024]{2,1,0:T(8,128)S(1)}, u32[]{:S(2)}, u32[]{:S(2)}) %collective-permute-start.1) | collective-permute-done | bytes 262176 | tf_op jit(solution)/shard_map/ppermute | solution.py:29
  200.1 15.6 %collective-permute-done.2 = f32[1,128,1024]{2,1,0:T(8,128)S(1)} collective-permute-done((f32[1,128,1024]{2,1,0:T(8,128)}, f32[1,128,1024]{2,1,0:T(8,128)S(1)}, u32[]{:S(2)}, u32[]{:S(2)}) %collective-permute-start.2) | collective-permute-done | bytes 524320 | tf_op jit(solution)/shard_map/ppermute | solution.py:29
  218.7 24.5 %collective-permute-done.3 = f32[1,256,1024]{2,1,0:T(8,128)} collective-permute-done((f32[1,256,1024]{2,1,0:T(8,128)}, f32[1,256,1024]{2,1,0:T(8,128)}, u32[]{:S(2)}, u32[]{:S(2)}) %collective-permute-start.3) | collective-permute-done | bytes 1048608 | tf_op jit(solution)/shard_map/ppermute | solution.py:29
  250.3 24.6 %collective-permute-done.4 = f32[1,512,1024]{2,1,0:T(8,128)} collective-permute-done((f32[1,512,1024]{2,1,0:T(8,128)}, f32[1,512,1024]{2,1,0:T(8,128)}, u32[]{:S(2)}, u32[]{:S(2)}) %collective-permute-start.4) | collective-permute-done | bytes 2097184 | tf_op jit(solution)/shard_map/ppermute | solution.py:29
  282.7 3.6 convolution_convert_fusion
  286.3 10.1 %fusion.11 = bf16[1,1024,1024]{2,1,0:T(8,128)(2,1)} fusion(bf16[1024,1024]{1,0:T(8,128)(2,1)} %convolution_convert_fusion, bf16[1024,1024]{1,0:T(8,128)(2,1)} %copy-done.4, f32[]{:T(128)} %bitcast.20), kind=kOutput, calls=%fused_computation.22 | convolution fusion | flops 4308598784 | bytes 6291460 | tf_op jit(solution)/shard_map/kij,kjl->kil/dot_general | solution.py:64
  300.3 14.3 %collective-permute-done.5 = bf16[1,512,1024]{2,1,0:T(8,128)(2,1)S(1)} collective-permute-done((bf16[1,512,1024]{2,1,0:T(8,128)(2,1)S(1)}, bf16[1,512,1024]{2,1,0:T(8,128)(2,1)S(1)}, u32[]{:S(2)}, u32[]{:S(2)}) %collective-permute-start.5) | collective-permute-done | bytes 1048608 | tf_op jit(solution)/shard_map/ppermute | solution.py:29
  315.2 8.9 %collective-permute-done.6 = bf16[1,256,1024]{2,1,0:T(8,128)(2,1)S(1)} collective-permute-done((bf16[1,256,1024]{2,1,0:T(8,128)(2,1)S(1)}, bf16[1,256,1024]{2,1,0:T(8,128)(2,1)S(1)}, u32[]{:S(2)}, u32[]{:S(2)}) %collective-permute-start.6) | collective-permute-done | bytes 524320 | tf_op jit(solution)/shard_map/ppermute | solution.py:29
  324.3 3.4 collective-permute-start.7
  327.7 7.1 %collective-permute-done.7 = bf16[1,128,1024]{2,1,0:T(8,128)(2,1)S(1)} collective-permute-done((bf16[1,128,1024]{2,1,0:T(8,128)(2,1)S(1)}, bf16[1,128,1024]{2,1,0:T(8,128)(2,1)S(1)}, u32[]{:S(2)}, u32[]{:S(2)}) %collective-permute-start.7) | collective-permute-done | bytes 262176 | tf_op jit(solution)/shard_map/ppermute | solution.py:29
  335.0 5.9 %collective-permute-done.8 = bf16[1,64,1024]{2,1,0:T(8,128)(2,1)S(1)} collective-permute-done((bf16[1,64,1024]{2,1,0:T(8,128)(2,1)S(1)}, bf16[1,64,1024]{2,1,0:T(8,128)(2,1)S(1)}, u32[]{:S(2)}, u32[]{:S(2)}) %collective-permute-start.8) | collective-permute-done | bytes 131104 | tf_op jit(solution)/shard_map/ppermute | solution.py:29
  348.4 11.1 %psum.28 = f32[]{:T(128)} all-reduce(f32[]{:T(128)} %multiply_reduce_fusion), channel_id=1, replica_groups=mesh['dp_0'=4,'dp_1'=8,'mp_0'=4,'mp_1'=2] {'dp_0'}, use_global_device_ids=true, to_apply=%region_4.0 | all-reduce | flops 1 | bytes 8 | tf_op jit(solution)/shard_map/psum | solution.py:22
  359.4 16.9 %psum.29 = f32[]{:T(128)} all-reduce(f32[]{:T(128)} %psum.28), channel_id=1, replica_groups=mesh['dp_0'=4,'dp_1'=8,'mp_0'=4,'mp_1'=2] {'dp_1'}, use_global_device_ids=true, to_apply=%region_5.0 | all-reduce | flops 1 | bytes 8 | tf_op jit(solution)/shard_map/psum | solution.py:22
  376.3 9.2 %psum.30 = f32[]{:T(128)} all-reduce(f32[]{:T(128)} %psum.29), channel_id=1, replica_groups=mesh['dp_0'=4,'dp_1'=8,'mp_0'=4,'mp_1'=2] {'mp_0'}, use_global_device_ids=true, to_apply=%region_6.0 | all-reduce | flops 1 | bytes 8 | tf_op jit(solution)/shard_map/psum | solution.py:22
  385.5 3.3 psum.31
  389.5 39.2 %all-gather.6.cloned.1.call-done = bf16[2097152]{0:T(1024)(128)(2,1)} async-done(((bf16[65536]{0:T(1024)(128)(2,1)}), bf16[2097152]{0:T(1024)(128)(2,1)}) %all-gather.6.cloned.1.call-update) | async-done | bytes 4194320 | tf_op jit(solution)/shard_map/all_gather | solution.py:40
  428.7 5.6 %reshape.643 = bf16[32,65536]{1,0:T(8,128)(2,1)} reshape(bf16[2097152]{0:T(1024)(128)(2,1)} %all-gather.6.cloned.1.call-done) | data formatting | bytes 8388608 | tf_op jit(solution)/shard_map/all_gather | solution.py:40
  434.3 3.8 fusion.51
  438.1 4.2 reshape.642
  444.7 5.9 %fusion.14 = bf16[1,1024,1024]{2,1,0:T(8,128)(2,1)} fusion(f32[]{:T(128)S(6)} %sqrt.3, bf16[1024,1024]{1,0:T(8,128)(2,1)} %reshape.641, bf16[1024,1024]{1,0:T(8,128)(2,1)} %reshape.642), kind=kOutput, calls=%fused_computation.23 | convolution fusion | flops 2149580800 | bytes 6291460 | tf_op jit(solution)/shard_map/brk,bkc->brc/dot_general | solution.py:142
  (80 shorter events, 43.1 us)
Async XLA Ops:
  7.2 157.9 %copy-start.10 = (f32[1,32,1024]{2,1,0:T(8,128)S(1)}, f32[1,32,1024]{2,1,0:T(8,128)}, u32[]{:S(2)}) copy-start(f32[1,32,1024]{2,1,0:T(8,128)} %param.7) | copy-start | bytes 393220
  7.2 38.6 %reduce-scatter.3.cloned.1.call-start = ((), (), s32[]{:S(2)}) async-start(), calls=%async_computation.2 | async-start | bytes 2621440 | tf_op jit(solution)/shard_map/reduce_scatter | solution.py:16
  7.2 160.4 %copy-start.11 = (f32[1,32,1024]{2,1,0:T(8,128)S(1)}, f32[1,32,1024]{2,1,0:T(8,128)}, u32[]{:S(2)}) copy-start(f32[1,32,1024]{2,1,0:T(8,128)} %param.8) | copy-start | bytes 393220
  7.9 77.9 %reduce-scatter.5.cloned.1.call-start = ((), (), s32[]{:S(2)}) async-start(), calls=%async_computation.3 | async-start | bytes 589824 | tf_op jit(solution)/shard_map/reduce_scatter | solution.py:16
  45.8 119.3 %all-gather.4.cloned.1.call-start = ((), (), s32[]{:S(2)}) async-start(), calls=%async_computation.4 | async-start | bytes 2162688 | tf_op jit(solution)/shard_map/all_gather | solution.py:84
  85.8 342.9 %all-gather.6.cloned.1.call-start = ((), (), s32[]{:S(2)}) async-start(), calls=%async_computation.5 | async-start | bytes 4325376 | tf_op jit(solution)/shard_map/all_gather | solution.py:40
  168.3 31.8 %copy-start.7 = (f32[1,32,1024]{2,1,0:T(8,128)}, f32[1,32,1024]{2,1,0:T(8,128)S(1)}, u32[]{:S(2)}) copy-start(f32[1,32,1024]{2,1,0:T(8,128)S(1)} %fusion.30) | copy-start | bytes 393220
  168.4 5.4 %collective-permute-start = (f32[1,32,1024]{2,1,0:T(8,128)S(1)}, f32[1,32,1024]{2,1,0:T(8,128)S(1)}, u32[]{:S(2)}, u32[]{:S(2)}) collective-permute-start(f32[1,32,1024]{2,1,0:T(8,128)S(1)} %get-tuple-element.9), channel_id=1, source_target_pairs={{0,8},{8,0},{16,24},{24,16},{32,40},{40,32},{48,56},{56,48},{64,72... | collective-permute-start | bytes 393224 | tf_op jit(solution)/shard_map/ppermute | solution.py:29
  174.5 21.7 %collective-permute-start.1 = (f32[1,64,1024]{2,1,0:T(8,128)}, f32[1,64,1024]{2,1,0:T(8,128)S(1)}, u32[]{:S(2)}, u32[]{:S(2)}) collective-permute-start(f32[1,64,1024]{2,1,0:T(8,128)} %maximum_select_fusion.8), channel_id=1, source_target_pairs={{0,16},{8,24},{16,0},{24,8},{32,48},{40,56},{48,32},{56,40},{64,80... | collective-permute-start | bytes 786440 | tf_op jit(solution)/shard_map/ppermute | solution.py:29
  197.1 18.6 %collective-permute-start.2 = (f32[1,128,1024]{2,1,0:T(8,128)}, f32[1,128,1024]{2,1,0:T(8,128)S(1)}, u32[]{:S(2)}, u32[]{:S(2)}) collective-permute-start(f32[1,128,1024]{2,1,0:T(8,128)} %maximum_select_fusion.6), channel_id=1, source_target_pairs={{0,32},{8,40},{16,48},{24,56},{32,0},{40,8},{48,16},{56,24},{64,96... | collective-permute-start | bytes 1572872 | tf_op jit(solution)/shard_map/ppermute | solution.py:29
  200.1 15.6 %copy-start.2 = (f32[128,1024]{1,0:T(8,128)}, f32[128,1024]{1,0:T(8,128)S(1)}, u32[]{:S(2)}) copy-start(f32[128,1024]{1,0:T(8,128)S(1)} %maximum_select_fusion.5) | copy-start | bytes 1572868
  216.8 26.3 %collective-permute-start.3 = (f32[1,256,1024]{2,1,0:T(8,128)}, f32[1,256,1024]{2,1,0:T(8,128)}, u32[]{:S(2)}, u32[]{:S(2)}) collective-permute-start(f32[1,256,1024]{2,1,0:T(8,128)} %maximum_select_fusion.4), channel_id=1, source_target_pairs={{0,64},{8,72},{16,80},{24,88},{32,96},{40,104},{48,112},{56,120},{... | collective-permute-start | bytes 3145736 | tf_op jit(solution)/shard_map/ppermute | solution.py:29
  246.4 28.5 %collective-permute-start.4 = (f32[1,512,1024]{2,1,0:T(8,128)}, f32[1,512,1024]{2,1,0:T(8,128)}, u32[]{:S(2)}, u32[]{:S(2)}) collective-permute-start(f32[1,512,1024]{2,1,0:T(8,128)} %maximum_select_fusion.2), channel_id=1, source_target_pairs={{0,128},{8,136},{16,144},{24,152},{32,160},{40,168},{48,176},{56,1... | collective-permute-start | bytes 6291464 | tf_op jit(solution)/shard_map/ppermute | solution.py:29
  296.4 18.2 %copy-start.1 = (bf16[1,1024,1024]{2,1,0:T(8,128)(2,1)S(1)}, bf16[1,1024,1024]{2,1,0:T(8,128)(2,1)}, u32[]{:S(2)}) copy-start(bf16[1,1024,1024]{2,1,0:T(8,128)(2,1)} %fusion.11) | copy-start | bytes 6291460
  298.2 16.4 %collective-permute-start.5 = (bf16[1,512,1024]{2,1,0:T(8,128)(2,1)S(1)}, bf16[1,512,1024]{2,1,0:T(8,128)(2,1)S(1)}, u32[]{:S(2)}, u32[]{:S(2)}) collective-permute-start(bf16[1,512,1024]{2,1,0:T(8,128)(2,1)S(1)} %broadcast_select_fusion), channel_id=1, source_target_pairs={{0,128},{8,136},{16,144},{24,152},{32,160},{40,168},{48,176},{56,1... | collective-permute-start | bytes 3145736 | tf_op jit(solution)/shard_map/ppermute | solution.py:29
  314.8 29.3 %copy-start.14 = (s32[1,2]{1,0:T(1,128)S(1)}, s32[1,2]{1,0:T(1,128)}, u32[]{:S(2)}) copy-start(s32[1,2]{1,0:T(1,128)} %param.11) | copy-start | bytes 28
  314.8 31.5 %copy-start.12 = (bf16[1,32,1024]{2,1,0:T(8,128)(2,1)S(1)}, bf16[1,32,1024]{2,1,0:T(8,128)(2,1)}, u32[]{:S(2)}) copy-start(bf16[1,32,1024]{2,1,0:T(8,128)(2,1)} %param.10) | copy-start | bytes 196612
  314.8 31.5 %copy-start.13 = (bf16[1,32,1024]{2,1,0:T(8,128)(2,1)S(1)}, bf16[1,32,1024]{2,1,0:T(8,128)(2,1)}, u32[]{:S(2)}) copy-start(bf16[1,32,1024]{2,1,0:T(8,128)(2,1)} %param.9) | copy-start | bytes 196612
  314.8 9.3 %collective-permute-start.6 = (bf16[1,256,1024]{2,1,0:T(8,128)(2,1)S(1)}, bf16[1,256,1024]{2,1,0:T(8,128)(2,1)S(1)}, u32[]{:S(2)}, u32[]{:S(2)}) collective-permute-start(bf16[1,256,1024]{2,1,0:T(8,128)(2,1)S(1)} %broadcast_select_fusion.1), channel_id=1, source_target_pairs={{0,64},{8,72},{16,80},{24,88},{32,96},{40,104},{48,112},{56,120},{... | collective-permute-start | bytes 1572872 | tf_op jit(solution)/shard_map/ppermute | solution.py:29
  324.3 10.5 %collective-permute-start.7 = (bf16[1,128,1024]{2,1,0:T(8,128)(2,1)S(1)}, bf16[1,128,1024]{2,1,0:T(8,128)(2,1)S(1)}, u32[]{:S(2)}, u32[]{:S(2)}) collective-permute-start(bf16[1,128,1024]{2,1,0:T(8,128)(2,1)S(1)} %broadcast_select_fusion.2), channel_id=1, source_target_pairs={{0,32},{8,40},{16,48},{24,56},{32,0},{40,8},{48,16},{56,24},{64,96... | collective-permute-start | bytes 786440 | tf_op jit(solution)/shard_map/ppermute | solution.py:29
  334.9 6.0 %collective-permute-start.8 = (bf16[1,64,1024]{2,1,0:T(8,128)(2,1)S(1)}, bf16[1,64,1024]{2,1,0:T(8,128)(2,1)S(1)}, u32[]{:S(2)}, u32[]{:S(2)}) collective-permute-start(bf16[1,64,1024]{2,1,0:T(8,128)(2,1)S(1)} %broadcast_select_fusion.3), channel_id=1, source_target_pairs={{0,16},{8,24},{16,0},{24,8},{32,48},{40,56},{48,32},{56,40},{64,80... | collective-permute-start | bytes 393224 | tf_op jit(solution)/shard_map/ppermute | solution.py:29
  340.9 5.4 %collective-permute-start.9 = (bf16[1,32,1024]{2,1,0:T(8,128)(2,1)S(1)}, bf16[1,32,1024]{2,1,0:T(8,128)(2,1)S(1)}, u32[]{:S(2)}, u32[]{:S(2)}) collective-permute-start(bf16[1,32,1024]{2,1,0:T(8,128)(2,1)S(1)} %get-tuple-element.13), channel_id=1, source_target_pairs={{0,8},{8,0},{16,24},{24,16},{32,40},{40,32},{48,56},{56,48},{64,72... | collective-permute-start | bytes 196616 | tf_op jit(solution)/shard_map/ppermute | solution.py:29
  346.5 87.8 %copy-start.8 = (bf16[1,32,1024]{2,1,0:T(8,128)(2,1)}, bf16[1,32,1024]{2,1,0:T(8,128)(2,1)S(1)}, u32[]{:S(2)}) copy-start(bf16[1,32,1024]{2,1,0:T(8,128)(2,1)S(1)} %get-tuple-element.10) | copy-start | bytes 196612
  346.5 87.8 %copy-start.9 = (bf16[1,32,1024]{2,1,0:T(8,128)(2,1)}, bf16[1,32,1024]{2,1,0:T(8,128)(2,1)S(1)}, u32[]{:S(2)}) copy-start(bf16[1,32,1024]{2,1,0:T(8,128)(2,1)S(1)} %get-tuple-element.11) | copy-start | bytes 196612
  (5 other events, 29.8 us)
Sparse Core Ops, SparseCore 0:
  10.5 35.2 reduce-scatter.2
  48.3 37.4 reduce-scatter.4
  88.4 76.6 all-gather.3
  347.8 80.8 all-gather.5
where the time goes:
time: 458 us; the launch traced here: 457 us
  waiting for transfers between devices  324 us (71%)
  blocking collectives  40.5 us (9%)
  matrix products  23.2 us (5%)
  other arithmetic  19.7 us (4%)
  starting transfers between devices  17.7 us (4%)
  local copies, waits for them, and re-layouts  16.1 us (4%)
  between operations  16.1 us (4%)
    ppermute x10, waiting for transfers between devices, swapped(): return lax.ppermute(value, axis, pairs)  127 us
    all_gather x1, waiting for transfers between devices, per_device(): full_grad = lax.all_gather(grad_rows, DP, axis=1, tiled=True)  79.2 us
    reduce_scatter x2, waiting for transfers between devices, scatter_axes(): value = lax.psum_scatter(value, axis, scatter_dimension=dim, tiled=True)  77.7 us
    psum x4, blocking collectives, by_axis(): value = lax.psum(value, axis)  40.5 us
    all_gather x1, waiting for transfers between devices, gather_packed(): lines, at, done = (lax.all_gather(ravelled, axis), 0, [])  39.2 us
    ppermute x10, starting transfers between devices, swapped(): return lax.ppermute(value, axis, pairs)  17.6 us
    dot_general x1, matrix products, root_batch(): jnp.einsum('kij,kjl->kil', fourth, combined, preferred_element_type=jnp.f...  10.1 us
    select_n x8, other arithmetic, per_device(): jnp.where(bit_value == 0, jnp.concatenate([kept_part, arrived], 1), jnp.c...  9.6 us
  transfers between devices with their start and end apart: 14, of which 14 were waited for; matrix products, arithmetic and copies ran while one was open for 1% of the time, Pallas kernels for 0%

commit v1 on v0

--- a/solution.py
+++ b/solution.py
@@ -1,3 +1,4 @@
+import functools
 import jax
 import jax.numpy as jnp
 from jax import lax
@@ -9,6 +10,16 @@
 MP = ("mp_0", "mp_1")
 epsilon = 1e-06
 decay = 0.9
+
+
+def lay_sizes_for(m, bus_axis):
+    outer = jax.lax.axis_size(bus_axis)
+    piece_out = jnp.stack(outer * [m], 0)
+    then = jax.lax.all_to_all(piece_out, bus_axis, 0, 0)
+    return jnp.concatenate(then, 1)
+
+
+wait_map_over_axis = functools.partial(lay_sizes_for, bus_axis=DP)
 
 
 def scatter_axes(value, axes, dim):
@@ -81,7 +92,7 @@
     grand_sum = by_axis(square_sum, DP_MP)
     entry_count = float(lax.axis_size(MP) * local_blocks * order_size * order_size)
     factor = 1.0 / jnp.sqrt(grand_sum / entry_count + epsilon)
-    full_grad = lax.all_gather(grad_rows, DP, axis=1, tiled=True)
+    full_grad = wait_map_over_axis(grad_rows)
     row_start = lax.axis_index(DP) * row_count
     own_cols = lax.dynamic_slice_in_dim(full_grad, row_start, row_count, 2)
     left_prod = jnp.einsum("brk,bck->brc", grad_rows, full_grad, preferred_element_type=jnp.float32)

time: 458 us -> 432 us (0.943)
  waiting for transfers between devices: 324 us -> 292 us
  starting transfers between devices: 17.7 us -> 22.9 us
    all_gather x1 -> x0, waiting for transfers between devices: 79.2 us -> none  [per_device(): full_grad = lax.all_gather(grad_rows, DP, axis=1, tiled=True)]
    all_to_all x0 -> x1, waiting for transfers between devices: none -> 46.5 us  [lay_sizes_for(): then = jax.lax.all_to_all(piece_out, bus_axis, 0, 0)]
    all_to_all x0 -> x1, starting transfers between devices: none -> 7.27 us  [lay_sizes_for(): then = jax.lax.all_to_all(piece_out, bus_axis, 0, 0)]
where the time goes in v1:
time: 432 us; the launch traced here: 431 us
  waiting for transfers between devices  292 us (68%)
  blocking collectives  41.1 us (10%)
  starting transfers between devices  22.9 us (5%)
  matrix products  21.4 us (5%)
  other arithmetic  19.6 us (5%)
  local copies, waits for them, and re-layouts  18.5 us (4%)
  between operations  16 us (4%)
    ppermute x10, waiting for transfers between devices, swapped(): return lax.ppermute(value, axis, pairs)  128 us
    reduce_scatter x2, waiting for transfers between devices, scatter_axes(): value = lax.psum_scatter(value, axis, scatter_dimension=dim, tiled=True)  77.8 us
    all_to_all x1, waiting for transfers between devices, lay_sizes_for(): then = jax.lax.all_to_all(piece_out, bus_axis, 0, 0)  46.5 us
    psum x4, blocking collectives, by_axis(): value = lax.psum(value, axis)  41.1 us
    all_gather x1, waiting for transfers between devices, gather_packed(): lines, at, done = (lax.all_gather(ravelled, axis), 0, [])  38.9 us
    ppermute x10, starting transfers between devices, swapped(): return lax.ppermute(value, axis, pairs)  15.5 us
    dot_general x1, matrix products, root_batch(): jnp.einsum('kij,kjl->kil', fourth, combined, preferred_element_type=jnp.f...  10.1 us
    select_n x8, other arithmetic, per_device(): jnp.where(bit_value == 0, jnp.concatenate([kept_part, arrived], 1), jnp.c...  9.52 us
  transfers between devices with their start and end apart: 14, of which 14 were waited for; matrix products, arithmetic and copies ran while one was open for 1% of the time, Pallas kernels for 0%

profile of v1, /device:TPU:2, one launch (start us, length us, event | category | flops | bytes accessed | tf_op | source)
XLA Modules:
  0.0 431.1 jit_solution(589060455234510422)
XLA Ops:
  7.9 37.8 %reduce-scatter.3.cloned.1.call-done = bf16[1,256,1024]{2,1,0:T(8,128)(2,1)} async-done(((bf16[1,1024,1024]{2,1,0:T(8,128)(2,1)}), bf16[1,256,1024]{2,1,0:T(8,128)(2,1)}) %reduce-scatter.3.cloned.1.call-update) | async-done | bytes 524304 | tf_op jit(solution)/shard_map/reduce_scatter | solution.py:27
  45.8 40.0 %reduce-scatter.5.cloned.1.call-done = bf16[1,32,1024]{2,1,0:T(8,128)(2,1)} async-done(((bf16[1,256,1024]{2,1,0:T(8,128)(2,1)}), bf16[1,32,1024]{2,1,0:T(8,128)(2,1)}) %reduce-scatter.5.cloned.1.call-update) | async-done | bytes 65552 | tf_op jit(solution)/shard_map/reduce_scatter | solution.py:27
  88.2 7.3 %all-to-all-start = ((bf16[32,1,32,1024]{3,2,1,0:T(8,128)(2,1)}), bf16[32,1,32,1024]{3,2,1,0:T(8,128)(2,1)S(1)}, u32[]{:S(2)}, u32[]{:S(2)}) async-start(bf16[32,1,32,1024]{3,2,1,0:T(8,128)(2,1)} %stack.6), calls=%async_computation.2 | async-start | bytes 4194304 | tf_op jit(solution)/shard_map/all_to_all | solution.py:18
  95.6 46.5 %all-to-all-done = bf16[32,1,32,1024]{3,2,1,0:T(8,128)(2,1)S(1)} async-done(((bf16[32,1,32,1024]{3,2,1,0:T(8,128)(2,1)}), bf16[32,1,32,1024]{3,2,1,0:T(8,128)(2,1)S(1)}, u32[]{:S(2)}, u32[]{:S(2)}) %all-to-all-start) | async-done | bytes 2097184 | tf_op jit(solution)/shard_map/all_to_all | solution.py:18
  144.7 4.6 %collective-permute-done = f32[1,32,1024]{2,1,0:T(8,128)S(1)} collective-permute-done((f32[1,32,1024]{2,1,0:T(8,128)S(1)}, f32[1,32,1024]{2,1,0:T(8,128)S(1)}, u32[]{:S(2)}, u32[]{:S(2)}) %collective-permute-start) | collective-permute-done | bytes 131104 | tf_op jit(solution)/shard_map/ppermute | solution.py:40
  151.8 19.8 %collective-permute-done.1 = f32[1,64,1024]{2,1,0:T(8,128)S(1)} collective-permute-done((f32[1,64,1024]{2,1,0:T(8,128)}, f32[1,64,1024]{2,1,0:T(8,128)S(1)}, u32[]{:S(2)}, u32[]{:S(2)}) %collective-permute-start.1) | collective-permute-done | bytes 262176 | tf_op jit(solution)/shard_map/ppermute | solution.py:40
  174.1 15.6 %collective-permute-done.2 = f32[1,128,1024]{2,1,0:T(8,128)S(1)} collective-permute-done((f32[1,128,1024]{2,1,0:T(8,128)}, f32[1,128,1024]{2,1,0:T(8,128)S(1)}, u32[]{:S(2)}, u32[]{:S(2)}) %collective-permute-start.2) | collective-permute-done | bytes 524320 | tf_op jit(solution)/shard_map/ppermute | solution.py:40
  193.9 23.3 %collective-permute-done.3 = f32[1,256,1024]{2,1,0:T(8,128)} collective-permute-done((f32[1,256,1024]{2,1,0:T(8,128)}, f32[1,256,1024]{2,1,0:T(8,128)}, u32[]{:S(2)}, u32[]{:S(2)}) %collective-permute-start.3) | collective-permute-done | bytes 1048608 | tf_op jit(solution)/shard_map/ppermute | solution.py:40
  225.3 24.1 %collective-permute-done.4 = f32[1,512,1024]{2,1,0:T(8,128)} collective-permute-done((f32[1,512,1024]{2,1,0:T(8,128)}, f32[1,512,1024]{2,1,0:T(8,128)}, u32[]{:S(2)}, u32[]{:S(2)}) %collective-permute-start.4) | collective-permute-done | bytes 2097184 | tf_op jit(solution)/shard_map/ppermute | solution.py:40
  257.2 3.6 convolution_convert_fusion
  260.9 10.1 %fusion.5 = bf16[1,1024,1024]{2,1,0:T(8,128)(2,1)} fusion(bf16[1024,1024]{1,0:T(8,128)(2,1)} %convolution_convert_fusion, bf16[1024,1024]{1,0:T(8,128)(2,1)} %copy-done.3, f32[]{:T(128)} %bitcast.21), kind=kOutput, calls=%fused_computation.16 | convolution fusion | flops 4308598784 | bytes 6291460 | tf_op jit(solution)/shard_map/kij,kjl->kil/dot_general | solution.py:75
  274.7 14.4 %collective-permute-done.5 = bf16[1,512,1024]{2,1,0:T(8,128)(2,1)S(1)} collective-permute-done((bf16[1,512,1024]{2,1,0:T(8,128)(2,1)S(1)}, bf16[1,512,1024]{2,1,0:T(8,128)(2,1)S(1)}, u32[]{:S(2)}, u32[]{:S(2)}) %collective-permute-start.5) | collective-permute-done | bytes 1048608 | tf_op jit(solution)/shard_map/ppermute | solution.py:40
  290.5 8.1 %collective-permute-done.6 = bf16[1,256,1024]{2,1,0:T(8,128)(2,1)S(1)} collective-permute-done((bf16[1,256,1024]{2,1,0:T(8,128)(2,1)S(1)}, bf16[1,256,1024]{2,1,0:T(8,128)(2,1)S(1)}, u32[]{:S(2)}, u32[]{:S(2)}) %collective-permute-start.6) | collective-permute-done | bytes 524320 | tf_op jit(solution)/shard_map/ppermute | solution.py:40
  302.1 7.1 %collective-permute-done.7 = bf16[1,128,1024]{2,1,0:T(8,128)(2,1)S(1)} collective-permute-done((bf16[1,128,1024]{2,1,0:T(8,128)(2,1)S(1)}, bf16[1,128,1024]{2,1,0:T(8,128)(2,1)S(1)}, u32[]{:S(2)}, u32[]{:S(2)}) %collective-permute-start.7) | collective-permute-done | bytes 262176 | tf_op jit(solution)/shard_map/ppermute | solution.py:40
  309.3 6.4 %collective-permute-done.8 = bf16[1,64,1024]{2,1,0:T(8,128)(2,1)S(1)} collective-permute-done((bf16[1,64,1024]{2,1,0:T(8,128)(2,1)S(1)}, bf16[1,64,1024]{2,1,0:T(8,128)(2,1)S(1)}, u32[]{:S(2)}, u32[]{:S(2)}) %collective-permute-start.8) | collective-permute-done | bytes 131104 | tf_op jit(solution)/shard_map/ppermute | solution.py:40
  315.9 4.2 collective-permute-done.9
  322.1 11.2 %psum.28 = f32[]{:T(128)} all-reduce(f32[]{:T(128)} %multiply_reduce_fusion), channel_id=1, replica_groups=mesh['dp_0'=4,'dp_1'=8,'mp_0'=4,'mp_1'=2] {'dp_0'}, use_global_device_ids=true, to_apply=%region_4.0 | all-reduce | flops 1 | bytes 8 | tf_op jit(solution)/shard_map/psum | solution.py:33
  333.3 17.6 %psum.29 = f32[]{:T(128)} all-reduce(f32[]{:T(128)} %psum.28), channel_id=1, replica_groups=mesh['dp_0'=4,'dp_1'=8,'mp_0'=4,'mp_1'=2] {'dp_1'}, use_global_device_ids=true, to_apply=%region_5.0 | all-reduce | flops 1 | bytes 8 | tf_op jit(solution)/shard_map/psum | solution.py:33
  350.9 9.0 %psum.30 = f32[]{:T(128)} all-reduce(f32[]{:T(128)} %psum.29), channel_id=1, replica_groups=mesh['dp_0'=4,'dp_1'=8,'mp_0'=4,'mp_1'=2] {'mp_0'}, use_global_device_ids=true, to_apply=%region_6.0 | all-reduce | flops 1 | bytes 8 | tf_op jit(solution)/shard_map/psum | solution.py:33
  363.8 38.9 %all-gather.3.cloned.1.call-done = bf16[2097152]{0:T(1024)(128)(2,1)} async-done(((bf16[65536]{0:T(1024)(128)(2,1)}), bf16[2097152]{0:T(1024)(128)(2,1)}) %all-gather.3.cloned.1.call-update) | async-done | bytes 4194320 | tf_op jit(solution)/shard_map/all_gather | solution.py:51
  402.8 5.6 %reshape.653 = bf16[32,65536]{1,0:T(8,128)(2,1)} reshape(bf16[2097152]{0:T(1024)(128)(2,1)} %all-gather.3.cloned.1.call-done) | data formatting | bytes 8388608 | tf_op jit(solution)/shard_map/all_gather | solution.py:51
  408.3 3.8 fusion.26
  412.1 4.2 reshape.652
  418.7 5.9 %fusion.8 = bf16[1,1024,1024]{2,1,0:T(8,128)(2,1)} fusion(f32[]{:T(128)S(6)} %sqrt.3, bf16[1024,1024]{1,0:T(8,128)(2,1)} %reshape.651, bf16[1024,1024]{1,0:T(8,128)(2,1)} %reshape.652), kind=kOutput, calls=%fused_computation.17 | convolution fusion | flops 2149580800 | bytes 6291460 | tf_op jit(solution)/shard_map/brk,bkc->brc/dot_general | solution.py:153
  (78 shorter events, 46.0 us)
Async XLA Ops:
  7.2 38.6 %reduce-scatter.3.cloned.1.call-start = ((), (), s32[]{:S(2)}) async-start(), calls=%async_computation.3 | async-start | bytes 2621440 | tf_op jit(solution)/shard_map/reduce_scatter | solution.py:27
  7.9 77.9 %reduce-scatter.5.cloned.1.call-start = ((), (), s32[]{:S(2)}) async-start(), calls=%async_computation.4 | async-start | bytes 589824 | tf_op jit(solution)/shard_map/reduce_scatter | solution.py:27
  88.2 53.8 %copy-start.9 = (f32[1,32,1024]{2,1,0:T(8,128)S(1)}, f32[1,32,1024]{2,1,0:T(8,128)}, u32[]{:S(2)}) copy-start(f32[1,32,1024]{2,1,0:T(8,128)} %param.8) | copy-start | bytes 393220
  88.2 53.8 %all-to-all-start = ((bf16[32,1,32,1024]{3,2,1,0:T(8,128)(2,1)}), bf16[32,1,32,1024]{3,2,1,0:T(8,128)(2,1)S(1)}, u32[]{:S(2)}, u32[]{:S(2)}) async-start(bf16[32,1,32,1024]{3,2,1,0:T(8,128)(2,1)} %stack.6), calls=%async_computation.2 | async-start | bytes 4194304 | tf_op jit(solution)/shard_map/all_to_all | solution.py:18
  95.5 47.2 %copy-start.4 = (bf16[1,32,1024]{2,1,0:T(8,128)(2,1)S(1)}, bf16[1,32,1024]{2,1,0:T(8,128)(2,1)}, u32[]{:S(2)}) copy-start(bf16[1,32,1024]{2,1,0:T(8,128)(2,1)} %reduce-scatter.5.cloned.1.call-done) | copy-start | bytes 196612
  95.5 47.2 %copy-start.10 = (f32[1,32,1024]{2,1,0:T(8,128)S(1)}, f32[1,32,1024]{2,1,0:T(8,128)}, u32[]{:S(2)}) copy-start(f32[1,32,1024]{2,1,0:T(8,128)} %param.7) | copy-start | bytes 393220
  95.5 307.3 %all-gather.3.cloned.1.call-start = ((), (), s32[]{:S(2)}) async-start(), calls=%async_computation.5 | async-start | bytes 4325376 | tf_op jit(solution)/shard_map/all_gather | solution.py:51
  143.4 30.7 %copy-start.6 = (f32[1,32,1024]{2,1,0:T(8,128)}, f32[1,32,1024]{2,1,0:T(8,128)S(1)}, u32[]{:S(2)}) copy-start(f32[1,32,1024]{2,1,0:T(8,128)S(1)} %fusion.12) | copy-start | bytes 393220
  143.5 5.8 %collective-permute-start = (f32[1,32,1024]{2,1,0:T(8,128)S(1)}, f32[1,32,1024]{2,1,0:T(8,128)S(1)}, u32[]{:S(2)}, u32[]{:S(2)}) collective-permute-start(f32[1,32,1024]{2,1,0:T(8,128)S(1)} %get-tuple-element.9), channel_id=1, source_target_pairs={{0,8},{8,0},{16,24},{24,16},{32,40},{40,32},{48,56},{56,48},{64,72... | collective-permute-start | bytes 393224 | tf_op jit(solution)/shard_map/ppermute | solution.py:40
  150.0 21.6 %collective-permute-start.1 = (f32[1,64,1024]{2,1,0:T(8,128)}, f32[1,64,1024]{2,1,0:T(8,128)S(1)}, u32[]{:S(2)}, u32[]{:S(2)}) collective-permute-start(f32[1,64,1024]{2,1,0:T(8,128)} %maximum_select_fusion.8), channel_id=1, source_target_pairs={{0,16},{8,24},{16,0},{24,8},{32,48},{40,56},{48,32},{56,40},{64,80... | collective-permute-start | bytes 786440 | tf_op jit(solution)/shard_map/ppermute | solution.py:40
  172.4 17.3 %collective-permute-start.2 = (f32[1,128,1024]{2,1,0:T(8,128)}, f32[1,128,1024]{2,1,0:T(8,128)S(1)}, u32[]{:S(2)}, u32[]{:S(2)}) collective-permute-start(f32[1,128,1024]{2,1,0:T(8,128)} %maximum_select_fusion.6), channel_id=1, source_target_pairs={{0,32},{8,40},{16,48},{24,56},{32,0},{40,8},{48,16},{56,24},{64,96... | collective-permute-start | bytes 1572872 | tf_op jit(solution)/shard_map/ppermute | solution.py:40
  190.9 26.3 %collective-permute-start.3 = (f32[1,256,1024]{2,1,0:T(8,128)}, f32[1,256,1024]{2,1,0:T(8,128)}, u32[]{:S(2)}, u32[]{:S(2)}) collective-permute-start(f32[1,256,1024]{2,1,0:T(8,128)} %maximum_select_fusion.4), channel_id=1, source_target_pairs={{0,64},{8,72},{16,80},{24,88},{32,96},{40,104},{48,112},{56,120},{... | collective-permute-start | bytes 3145736 | tf_op jit(solution)/shard_map/ppermute | solution.py:40
  220.5 28.9 %collective-permute-start.4 = (f32[1,512,1024]{2,1,0:T(8,128)}, f32[1,512,1024]{2,1,0:T(8,128)}, u32[]{:S(2)}, u32[]{:S(2)}) collective-permute-start(f32[1,512,1024]{2,1,0:T(8,128)} %maximum_select_fusion.2), channel_id=1, source_target_pairs={{0,128},{8,136},{16,144},{24,152},{32,160},{40,168},{48,176},{56,1... | collective-permute-start | bytes 6291464 | tf_op jit(solution)/shard_map/ppermute | solution.py:40
  270.9 18.2 %copy-start = (bf16[1,1024,1024]{2,1,0:T(8,128)(2,1)S(1)}, bf16[1,1024,1024]{2,1,0:T(8,128)(2,1)}, u32[]{:S(2)}) copy-start(bf16[1,1024,1024]{2,1,0:T(8,128)(2,1)} %fusion.5) | copy-start | bytes 6291460
  272.7 16.4 %collective-permute-start.5 = (bf16[1,512,1024]{2,1,0:T(8,128)(2,1)S(1)}, bf16[1,512,1024]{2,1,0:T(8,128)(2,1)S(1)}, u32[]{:S(2)}, u32[]{:S(2)}) collective-permute-start(bf16[1,512,1024]{2,1,0:T(8,128)(2,1)S(1)} %broadcast_select_fusion), channel_id=1, source_target_pairs={{0,128},{8,136},{16,144},{24,152},{32,160},{40,168},{48,176},{56,1... | collective-permute-start | bytes 3145736 | tf_op jit(solution)/shard_map/ppermute | solution.py:40
  289.3 26.6 %copy-start.13 = (s32[1,2]{1,0:T(1,128)S(1)}, s32[1,2]{1,0:T(1,128)}, u32[]{:S(2)}) copy-start(s32[1,2]{1,0:T(1,128)} %param.11) | copy-start | bytes 28
  289.3 30.8 %copy-start.11 = (bf16[1,32,1024]{2,1,0:T(8,128)(2,1)S(1)}, bf16[1,32,1024]{2,1,0:T(8,128)(2,1)}, u32[]{:S(2)}) copy-start(bf16[1,32,1024]{2,1,0:T(8,128)(2,1)} %param.10) | copy-start | bytes 196612
  289.4 30.8 %copy-start.12 = (bf16[1,32,1024]{2,1,0:T(8,128)(2,1)S(1)}, bf16[1,32,1024]{2,1,0:T(8,128)(2,1)}, u32[]{:S(2)}) copy-start(bf16[1,32,1024]{2,1,0:T(8,128)(2,1)} %param.9) | copy-start | bytes 196612
  289.4 9.3 %collective-permute-start.6 = (bf16[1,256,1024]{2,1,0:T(8,128)(2,1)S(1)}, bf16[1,256,1024]{2,1,0:T(8,128)(2,1)S(1)}, u32[]{:S(2)}, u32[]{:S(2)}) collective-permute-start(bf16[1,256,1024]{2,1,0:T(8,128)(2,1)S(1)} %broadcast_select_fusion.1), channel_id=1, source_target_pairs={{0,64},{8,72},{16,80},{24,88},{32,96},{40,104},{48,112},{56,120},{... | collective-permute-start | bytes 1572872 | tf_op jit(solution)/shard_map/ppermute | solution.py:40
  298.8 10.4 %collective-permute-start.7 = (bf16[1,128,1024]{2,1,0:T(8,128)(2,1)S(1)}, bf16[1,128,1024]{2,1,0:T(8,128)(2,1)S(1)}, u32[]{:S(2)}, u32[]{:S(2)}) collective-permute-start(bf16[1,128,1024]{2,1,0:T(8,128)(2,1)S(1)} %broadcast_select_fusion.2), channel_id=1, source_target_pairs={{0,32},{8,40},{16,48},{24,56},{32,0},{40,8},{48,16},{56,24},{64,96... | collective-permute-start | bytes 786440 | tf_op jit(solution)/shard_map/ppermute | solution.py:40
  309.2 6.5 %collective-permute-start.8 = (bf16[1,64,1024]{2,1,0:T(8,128)(2,1)S(1)}, bf16[1,64,1024]{2,1,0:T(8,128)(2,1)S(1)}, u32[]{:S(2)}, u32[]{:S(2)}) collective-permute-start(bf16[1,64,1024]{2,1,0:T(8,128)(2,1)S(1)} %broadcast_select_fusion.3), channel_id=1, source_target_pairs={{0,16},{8,24},{16,0},{24,8},{32,48},{40,56},{48,32},{56,40},{64,80... | collective-permute-start | bytes 393224 | tf_op jit(solution)/shard_map/ppermute | solution.py:40
  315.8 4.4 %collective-permute-start.9 = (bf16[1,32,1024]{2,1,0:T(8,128)(2,1)S(1)}, bf16[1,32,1024]{2,1,0:T(8,128)(2,1)S(1)}, u32[]{:S(2)}, u32[]{:S(2)}) collective-permute-start(bf16[1,32,1024]{2,1,0:T(8,128)(2,1)S(1)} %get-tuple-element.13), channel_id=1, source_target_pairs={{0,8},{8,0},{16,24},{24,16},{32,40},{40,32},{48,56},{56,48},{64,72... | collective-permute-start | bytes 196616 | tf_op jit(solution)/shard_map/ppermute | solution.py:40
  320.2 88.1 %copy-start.7 = (bf16[1,32,1024]{2,1,0:T(8,128)(2,1)}, bf16[1,32,1024]{2,1,0:T(8,128)(2,1)S(1)}, u32[]{:S(2)}) copy-start(bf16[1,32,1024]{2,1,0:T(8,128)(2,1)S(1)} %get-tuple-element.10) | copy-start | bytes 196612
  320.3 88.1 %copy-start.8 = (bf16[1,32,1024]{2,1,0:T(8,128)(2,1)}, bf16[1,32,1024]{2,1,0:T(8,128)(2,1)S(1)}, u32[]{:S(2)}) copy-start(bf16[1,32,1024]{2,1,0:T(8,128)(2,1)S(1)} %get-tuple-element.11) | copy-start | bytes 196612
  (4 other events, 30.9 us)
Sparse Core Ops, SparseCore 0:
  10.5 35.2 reduce-scatter.2
  48.3 37.4 reduce-scatter.4
  321.6 81.1 all-gather.2
